TPU v7x, 32 devices: a whole 2x2x4 slice. The times are simulated.
32 devices in a mesh: groups: 2 (over y), assets: 8 (over z, x), tm: 2 (over core).
Axes of the slice: x: 2, y: 2, z: 4, core: 2. Of those that a mesh axis runs over, the one named last changes fastest.
Arguments:
- returns: bfloat16 [1536, 16384], P('tm', ('groups', 'assets')), parts along dimension 1, may hold values from -24 to 24
- prior: float32 [16384, 8192], P(('groups', 'assets')), parts along dimension 0, may hold values from -3 to 3
Outputs:
- covariance: float32 [2, 16384, 8192], P('tm', ('groups', 'assets')), parts along dimension 1
There are 2 independent parts, one for each index of `groups`. A program takes and returns all parts, laid end to end along the dimension named above; each array names one. Nothing has to cross between parts.
All inputs are finite; a program needn't handle non-finite values.
Results may differ from a plain program's by a relative error of at most 0.0045.
Values may be sent and summed in bfloat16 or wider, within the bound.
A program may use at most 256 MiB of HBM per device.

v0:
```python
import functools

import jax
import jax.numpy as jnp
from jax import lax
from jax.experimental import pallas as pl
from jax.experimental.pallas import tpu as pltpu
from jax.sharding import PartitionSpec as P

MESH = pl.DeviceIdType.MESH
PIECES = 4


def powers_of(minutes):
    lam = jnp.float32(0.9995)
    position = jnp.arange(minutes, dtype=jnp.float32)
    square = (jnp.float32(1.0) - lam) * jnp.power(lam, jnp.float32(minutes - 1) - position)
    return square, jnp.power(lam, jnp.float32(minutes))


def local_general(returns, prior):
    minutes, _ = returns.shape
    square, factor = powers_of(minutes)
    scaled = (returns.astype(jnp.float32) * jnp.sqrt(square)[:, None]).astype(jnp.bfloat16)
    tile = lax.dot_general(
        scaled,
        lax.all_gather(scaled, "assets", axis=1, tiled=True),
        (((0,), (0,)), ((), ())),
        preferred_element_type=jnp.float32,
    )
    mine = lax.axis_index("tm")
    everything = lax.all_gather(tile.astype(jnp.bfloat16), "tm")

    def turn(k, before):
        new = factor * before + everything[k].astype(jnp.float32)
        return jnp.where(k < mine, new, before)

    before = lax.fori_loop(0, lax.axis_size("tm"), turn, prior)
    return (factor * before + tile)[None]


def kernel(
    coef, returns, prior, square, total, mine, early, left, left_early,
    load_sem, prior_sem, x_send, z_send, c_send, f_send, x_recv, z_recv, c_recv, f_recv
):
    minutes, width = returns.shape
    part = width // PIECES
    me, core = lax.axis_index("assets"), lax.axis_index("tm")
    row, column = me // 2, me % 2
    other = 1 - column
    upper = row // 2
    outer = jnp.logical_or(row == 0, row == 3)
    inner = jnp.logical_not(outer)
    first, second = core == 0, core == 1
    line_row = lambda q: q + upper * (3 - 2 * q)
    block = lambda q, c: line_row(q) * 2 + c
    depth = (1 - upper) * row + upper * (3 - row)
    across = row * 2 + other
    beside = block(1 - depth, column)
    centre = (3 - row) * 2 + column

    barrier = pltpu.get_barrier_semaphore()
    for there in (across, beside):
        pl.semaphore_signal(barrier, 1, device_id={"assets": there}, device_id_type=MESH)
    pl.semaphore_signal(barrier, 1, device_id={"tm": 1 - core}, device_id_type=MESH)

    @pl.when(inner)
    def _():
        pl.semaphore_signal(barrier, 1, device_id={"assets": centre}, device_id_type=MESH)
        pl.semaphore_wait(barrier, 4)

    @pl.when(outer)
    def _():
        pl.semaphore_wait(barrier, 3)

    def remote(source, target, send, recv, where):
        return pltpu.make_async_remote_copy(
            src_ref=source, dst_ref=target, send_sem=send, recv_sem=recv,
            device_id=where, device_id_type=MESH,
        )

    def slot(j, p):
        return mine.at[j * PIECES + p]

    def send_x(source, j, p, k):
        remote(source, slot(j, p), x_send.at[k], x_recv.at[k], {"assets": across}).start()

    def send_z(source, j, p, k):
        remote(source, slot(j, p), z_send.at[k], z_recv.at[k], {"assets": beside}).start()

    def send_c(source, j, p, k):
        remote(source, slot(j, p), c_send.at[k], c_recv.at[k], {"assets": centre}).start()

    def hand_on(source, j, p):
        k = j * PIECES + p

        @pl.when(first)
        def _():
            remote(source, early.at[k], f_send.at[k], f_recv.at[k], {"tm": 1 - core}).start()

    def wait_recv(sem):
        pltpu.make_async_copy(mine.at[0], mine.at[0], sem).wait()

    def got(sem, j, p):
        wait_recv(sem)
        hand_on(slot(j, p), j, p)

    own = lambda p: returns.at[:, pl.ds(p * part, part)]

    for p in range(PIECES):
        send_x(own(p), me, p, p)
        send_z(own(p), me, p, p)

        @pl.when(inner)
        def _():
            send_c(own(p), me, p, p)

        hand_on(own(p), me, p)
        pltpu.make_async_copy(own(p), slot(me, p), load_sem.at[p]).start()

    blocks = total.shape[1] // width

    def prior_copy(j):
        columns = pl.ds(pl.multiple_of(j * width, width), width)
        return pltpu.make_async_copy(prior.at[:, columns], total.at[:, columns], prior_sem.at[j])

    def start_prior(j, carry):
        prior_copy(j).start()
        return carry

    lax.fori_loop(0, blocks, start_prior, 0)

    def prepare(p, carry):
        pltpu.make_async_copy(own(p), slot(me, p), load_sem.at[p]).wait()
        rows = pl.ds(pl.multiple_of(p * part, part), part)
        turned = mine[me * PIECES + p].astype(jnp.float32).T
        left[rows, :] = (turned * square[...]).astype(jnp.bfloat16)

        @pl.when(second)
        def _():
            k = me * PIECES + p
            wait_recv(f_recv.at[k])
            turned = early[k].astype(jnp.float32).T
            left_early[rows, :] = (turned * (coef[1] * square[...])).astype(jnp.bfloat16)

        return carry

    lax.fori_loop(0, PIECES, prepare, 0)

    def wait_prior(j, carry):
        prior_copy(j).wait()
        return carry

    lax.fori_loop(0, blocks, wait_prior, 0)

    def product(j, p, arrived=True):
        k = j * PIECES + p
        columns = pl.ds(pl.multiple_of(j * width + p * part, part), part)

        @pl.when(first)
        def _():
            total[:, columns] = coef[0] * total[:, columns] + jnp.dot(
                left[...], mine[k], preferred_element_type=jnp.float32
            )

        @pl.when(second)
        def _():
            if arrived:
                wait_recv(f_recv.at[k])
            total[:, columns] = (
                coef[0] * total[:, columns]
                + jnp.dot(left[...], mine[k], preferred_element_type=jnp.float32)
                + jnp.dot(left_early[...], early[k], preferred_element_type=jnp.float32)
            )

    def own_product(p, carry):
        product(me, p, arrived=False)
        return carry

    lax.fori_loop(0, PIECES, own_product, 0)

    @pl.when(outer)
    def _():
        def turn(k, carry):
            q, p = k // PIECES, k % PIECES
            jx, jz = block(q, other), block(1 + q, column)
            got(x_recv.at[k], jx, p)

            @pl.when(q == 0)
            def _():
                send_z(slot(jx, p), jx, p, PIECES + k)

            got(z_recv.at[k], jz, p)

            @pl.when(k < 10)
            def _():
                send_x(slot(jz, p), jz, p, PIECES + k)

            product(jx, p)
            product(jz, p)
            return carry

        lax.fori_loop(0, 3 * PIECES, turn, 0)

        def end(p, carry):
            j = block(3, other)
            got(x_recv.at[12 + p], j, p)
            got(z_recv.at[12 + p], j, 2 + p)
            product(j, p)
            product(j, 2 + p)
            return carry

        lax.fori_loop(0, 2, end, 0)

    @pl.when(inner)
    def _():
        def turn(k, carry):
            q, p = k // PIECES, k % PIECES
            jx, jz, jc = block(1 + q, other), block(0, (column + q) % 2), block(2 + q, column)
            got(c_recv.at[k], jc, p)
            send_z(slot(jc, p), jc, p, PIECES + k)
            send_x(slot(jc, p), jc, p, PIECES + k + q * (2 - 4 * (p // 2)))
            got(z_recv.at[k], jz, p)

            @pl.when(q == 0)
            def _():
                send_c(slot(jz, p), jz, p, PIECES + k)

            got(x_recv.at[k], jx, p)
            product(jc, p)
            product(jz, p)
            product(jx, p)
            return carry

        lax.fori_loop(0, 2 * PIECES, turn, 0)

        def end(k, carry):
            j, p = block(3, other), (k + 2) % PIECES
            got(x_recv.at[2 * PIECES + k], j, p)

            @pl.when(k < 2)
            def _():
                send_z(slot(j, p), j, p, 3 * PIECES + k)

            product(j, p)
            return carry

        lax.fori_loop(0, PIECES, end, 0)

    def wait_send(sem):
        pltpu.make_async_copy(mine.at[0], mine.at[0], sem).wait()

    def waits(sems, count):
        def turn(k, carry):
            wait_send(sems.at[k])
            return carry

        lax.fori_loop(0, count, turn, 0)

    @pl.when(outer)
    def _():
        waits(x_send, 14)
        waits(z_send, 8)

    @pl.when(inner)
    def _():
        waits(x_send, 12)
        waits(z_send, 14)
        waits(c_send, 8)

    @pl.when(first)
    def _():
        waits(f_send, blocks * PIECES)


def local_planned(returns, prior):
    minutes, width = returns.shape
    rows, assets = prior.shape
    part = width // PIECES
    square, factor = powers_of(minutes)
    slab = lax.axis_index("tm")
    coef = jnp.stack([jnp.where(slab > 0, factor * factor, factor), factor])
    count = assets // width * PIECES
    out = pl.pallas_call(
        kernel,
        out_shape=pltpu.VMEM((rows, assets), jnp.float32),
        in_specs=[
            pl.BlockSpec(memory_space=pltpu.SMEM),
            pl.BlockSpec(memory_space=pltpu.HBM),
            pl.BlockSpec(memory_space=pltpu.HBM),
            pl.BlockSpec(memory_space=pltpu.VMEM),
        ],
        out_specs=pl.BlockSpec(memory_space=pltpu.VMEM),
        scratch_shapes=[
            pltpu.VMEM((count, minutes, part), jnp.bfloat16),
            pltpu.VMEM((count, minutes, part), jnp.bfloat16),
            pltpu.VMEM((width, minutes), jnp.bfloat16),
            pltpu.VMEM((width, minutes), jnp.bfloat16),
            pltpu.SemaphoreType.DMA((PIECES,)),
            pltpu.SemaphoreType.DMA((assets // width,)),
            pltpu.SemaphoreType.DMA((14,)),
            pltpu.SemaphoreType.DMA((14,)),
            pltpu.SemaphoreType.DMA((8,)),
            pltpu.SemaphoreType.DMA((count,)),
            pltpu.SemaphoreType.DMA((14,)),
            pltpu.SemaphoreType.DMA((14,)),
            pltpu.SemaphoreType.DMA((8,)),
            pltpu.SemaphoreType.DMA((count,)),
        ],
        compiler_params=pltpu.CompilerParams(
            collective_id=0, has_side_effects=True, vmem_limit_bytes=31457280
        ),
    )(coef, pltpu.with_memory_space_constraint(returns, pltpu.HBM), prior, square[None, :])
    return out[None]


def solution(mesh):
    placed = (P("tm", ("groups", "assets")), P(("groups", "assets"), None))
    planned = mesh.shape["tm"] == 2 and mesh.shape["assets"] == 8

    def local(returns, prior):
        if planned and returns.shape[1] % (128 * PIECES) == 0 and returns.shape[0] % 128 == 0:
            return local_planned(returns, prior)
        return local_general(returns, prior)

    return jax.shard_map(
        local,
        mesh=mesh,
        in_specs=placed,
        out_specs=P("tm", ("groups", "assets"), None),
        check_vma=False,
    )
```

profile of v0, /device:TPU:1, one launch (start us, length us, event | category | flops | bytes accessed | tf_op | source)
XLA Modules:
  0.0 141.5 jit_solution(17973502278611272877)
XLA Ops:
  0.0 0.7 pad_maximum_fusion.coef
  0.7 0.6 power_multiply_fusion.square
  1.3 128.6 %shard_map.28 = f32[1024,8192]{1,0:T(8,128)S(1)} custom-call(f32[2]{0:T(128)} %pad_maximum_fusion.coef, bf16[768,1024]{1,0:T(8,128)(2,1)} %returns.1, f32[1024,8192]{1,0:T(8,128)} %prior.1, f32[1,768]{1,0:T(1,128)} %power_multiply_fusion.square), custom_call_target="tpu_custom_call" | custom-call | tf_op jit(solution)/shard_map/pallas_call | solution.py:284
  129.8 11.7 %copy.4 = f32[1,1024,8192]{2,1,0:T(8,128)} copy(f32[1,1024,8192]{2,1,0:T(8,128)S(1)} %bitcast.2) | data formatting | bytes 67108864
where the time goes:
time: 142 us
  Pallas kernels  129 us (91%)
  local copies, waits for them, and re-layouts  11.7 us (8%)
    pallas_call x1, Pallas kernels, local_planned(): pl.pallas_call(kernel, out_shape=pltpu.VMEM((rows, assets), jnp.float32),...  129 us
    unnamed x1, local copies, waits for them, and re-layouts  11.7 us

commit v1 on v0

--- a/solution.py
+++ b/solution.py
@@ -1,7 +1,9 @@
 import functools
+import math
 
 import jax
 import jax.numpy as jnp
+import numpy as np
 from jax import lax
 from jax.experimental import pallas as pl
 from jax.experimental.pallas import tpu as pltpu
@@ -9,6 +11,7 @@
 
 MESH = pl.DeviceIdType.MESH
 PIECES = 4
+HALF = PIECES // 2
 
 
 def powers_of(minutes):
@@ -40,7 +43,7 @@
 
 
 def kernel(
-    coef, returns, prior, square, total, mine, early, left, left_early,
+    returns, prior, total, tail, left, hand, mine, early, left_early,
     load_sem, prior_sem, x_send, z_send, c_send, f_send, x_recv, z_recv, c_recv, f_recv
 ):
     minutes, width = returns.shape
@@ -52,6 +55,10 @@
     outer = jnp.logical_or(row == 0, row == 3)
     inner = jnp.logical_not(outer)
     first, second = core == 0, core == 1
+    lam = float(np.float32(0.9995))
+    factor = lam**minutes
+    age = (minutes - 1) - lax.broadcasted_iota(jnp.int32, (1, minutes), 1)
+    square = (1.0 - lam) * jnp.exp(age.astype(jnp.float32) * math.log(lam))
     line_row = lambda q: q + upper * (3 - 2 * q)
     block = lambda q, c: line_row(q) * 2 + c
     depth = (1 - upper) * row + upper * (3 - row)
@@ -118,30 +125,38 @@
         hand_on(own(p), me, p)
         pltpu.make_async_copy(own(p), slot(me, p), load_sem.at[p]).start()
 
-    blocks = total.shape[1] // width
-
-    def prior_copy(j):
+    blocks = prior.shape[1] // width
+    last = block(3, other)
+    place_of = lambda j: (j + blocks - 1 - last) % blocks
+
+    def prior_copy(k):
+        j = (last + 1 + k) % blocks
         columns = pl.ds(pl.multiple_of(j * width, width), width)
-        return pltpu.make_async_copy(prior.at[:, columns], total.at[:, columns], prior_sem.at[j])
-
-    def start_prior(j, carry):
-        prior_copy(j).start()
+        return pltpu.make_async_copy(prior.at[:, columns], total.at[k], prior_sem.at[k])
+
+    tail_copy = pltpu.make_async_copy(
+        prior.at[:, pl.ds(pl.multiple_of(last * width, width), width)], tail, prior_sem.at[blocks - 1]
+    )
+
+    def start_prior(k, carry):
+        prior_copy(k).start()
         return carry
 
-    lax.fori_loop(0, blocks, start_prior, 0)
+    lax.fori_loop(0, blocks - 1, start_prior, 0)
+    tail_copy.start()
 
     def prepare(p, carry):
         pltpu.make_async_copy(own(p), slot(me, p), load_sem.at[p]).wait()
         rows = pl.ds(pl.multiple_of(p * part, part), part)
         turned = mine[me * PIECES + p].astype(jnp.float32).T
-        left[rows, :] = (turned * square[...]).astype(jnp.bfloat16)
+        left[rows, :] = (turned * square).astype(jnp.bfloat16)
 
         @pl.when(second)
         def _():
             k = me * PIECES + p
             wait_recv(f_recv.at[k])
             turned = early[k].astype(jnp.float32).T
-            left_early[rows, :] = (turned * (coef[1] * square[...])).astype(jnp.bfloat16)
+            left_early[rows, :] = (turned * (factor * square)).astype(jnp.bfloat16)
 
         return carry
 
@@ -151,15 +166,19 @@
         prior_copy(j).wait()
         return carry
 
-    lax.fori_loop(0, blocks, wait_prior, 0)
-
-    def product(j, p, arrived=True):
+    lax.fori_loop(0, blocks - 1, wait_prior, 0)
+    tail_copy.wait()
+
+    def keep(j, p, k):
+        return pltpu.make_async_copy(slot(j, p), hand.at[k], load_sem.at[k])
+
+    def product(target, j, p, arrived=True, whole=True):
         k = j * PIECES + p
-        columns = pl.ds(pl.multiple_of(j * width + p * part, part), part)
+        columns = pl.ds(pl.multiple_of(p * part, part), part)
 
         @pl.when(first)
         def _():
-            total[:, columns] = coef[0] * total[:, columns] + jnp.dot(
+            target[:, columns] = factor * target[:, columns] + jnp.dot(
                 left[...], mine[k], preferred_element_type=jnp.float32
             )
 
@@ -167,14 +186,15 @@
         def _():
             if arrived:
                 wait_recv(f_recv.at[k])
-            total[:, columns] = (
-                coef[0] * total[:, columns]
-                + jnp.dot(left[...], mine[k], preferred_element_type=jnp.float32)
-                + jnp.dot(left_early[...], early[k], preferred_element_type=jnp.float32)
+            now = factor * factor * target[:, columns] + jnp.dot(
+                left_early[...], early[k], preferred_element_type=jnp.float32
             )
+            if whole:
+                now += jnp.dot(left[...], mine[k], preferred_element_type=jnp.float32)
+            target[:, columns] = now
 
     def own_product(p, carry):
-        product(me, p, arrived=False)
+        product(total.at[place_of(me)], me, p, arrived=False)
         return carry
 
     lax.fori_loop(0, PIECES, own_product, 0)
@@ -191,26 +211,35 @@
                 send_z(slot(jx, p), jx, p, PIECES + k)
 
             got(z_recv.at[k], jz, p)
-
-            @pl.when(k < 10)
+            late = jnp.logical_and(k >= 2 * PIECES, k < 2 * PIECES + HALF)
+
+            @pl.when(jnp.logical_or(k < 2 * PIECES, jnp.logical_and(late, first)))
             def _():
                 send_x(slot(jz, p), jz, p, PIECES + k)
 
-            product(jx, p)
-            product(jz, p)
+            @pl.when(jnp.logical_and(late, second))
+            def _():
+                keep(jz, p, p).start()
+
+            product(total.at[place_of(jx)], jx, p)
+            product(total.at[place_of(jz)], jz, p)
             return carry
 
         lax.fori_loop(0, 3 * PIECES, turn, 0)
 
         def end(p, carry):
             j = block(3, other)
-            got(x_recv.at[12 + p], j, p)
-            got(z_recv.at[12 + p], j, 2 + p)
-            product(j, p)
-            product(j, 2 + p)
+
+            @pl.when(first)
+            def _():
+                got(x_recv.at[3 * PIECES + p], j, p)
+                got(z_recv.at[3 * PIECES + p], j, HALF + p)
+
+            product(tail, j, p, whole=False)
+            product(tail, j, HALF + p, whole=False)
             return carry
 
-        lax.fori_loop(0, 2, end, 0)
+        lax.fori_loop(0, HALF, end, 0)
 
     @pl.when(inner)
     def _():
@@ -219,7 +248,7 @@
             jx, jz, jc = block(1 + q, other), block(0, (column + q) % 2), block(2 + q, column)
             got(c_recv.at[k], jc, p)
             send_z(slot(jc, p), jc, p, PIECES + k)
-            send_x(slot(jc, p), jc, p, PIECES + k + q * (2 - 4 * (p // 2)))
+            send_x(slot(jc, p), jc, p, PIECES + k + q * HALF * (1 - 2 * (p // HALF)))
             got(z_recv.at[k], jz, p)
 
             @pl.when(q == 0)
@@ -227,22 +256,26 @@
                 send_c(slot(jz, p), jz, p, PIECES + k)
 
             got(x_recv.at[k], jx, p)
-            product(jc, p)
-            product(jz, p)
-            product(jx, p)
+            product(total.at[place_of(jc)], jc, p)
+            product(total.at[place_of(jz)], jz, p)
+            product(total.at[place_of(jx)], jx, p)
             return carry
 
         lax.fori_loop(0, 2 * PIECES, turn, 0)
 
         def end(k, carry):
-            j, p = block(3, other), (k + 2) % PIECES
+            j, p = block(3, other), (k + HALF) % PIECES
             got(x_recv.at[2 * PIECES + k], j, p)
 
-            @pl.when(k < 2)
+            @pl.when(jnp.logical_and(k < HALF, first))
             def _():
                 send_z(slot(j, p), j, p, 3 * PIECES + k)
 
-            product(j, p)
+            @pl.when(jnp.logical_and(k < HALF, second))
+            def _():
+                keep(j, p, k).start()
+
+            product(tail, j, p)
             return carry
 
         lax.fori_loop(0, PIECES, end, 0)
@@ -250,68 +283,156 @@
     def wait_send(sem):
         pltpu.make_async_copy(mine.at[0], mine.at[0], sem).wait()
 
-    def waits(sems, count):
+    def waits(sems, start, stop):
         def turn(k, carry):
             wait_send(sems.at[k])
             return carry
 
-        lax.fori_loop(0, count, turn, 0)
-
-    @pl.when(outer)
-    def _():
-        waits(x_send, 14)
-        waits(z_send, 8)
+        lax.fori_loop(start, stop, turn, 0)
+
+    waits(x_send, 0, 3 * PIECES)
+    waits(z_send, 0, 2 * PIECES)
 
     @pl.when(inner)
     def _():
-        waits(x_send, 12)
-        waits(z_send, 14)
-        waits(c_send, 8)
+        waits(z_send, 2 * PIECES, 3 * PIECES)
+        waits(c_send, 0, 2 * PIECES)
 
     @pl.when(first)
     def _():
-        waits(f_send, blocks * PIECES)
+        pl.when(outer)(lambda: waits(x_send, 3 * PIECES, 3 * PIECES + HALF))
+        pl.when(inner)(lambda: waits(z_send, 3 * PIECES, 3 * PIECES + HALF))
+        waits(f_send, 0, blocks * PIECES)
+
+    @pl.when(second)
+    def _():
+        for k in range(HALF):
+            keep(0, 0, k).wait()
+
+
+def place():
+    me = lax.axis_index("assets")
+    row, column = me // 2, me % 2
+    upper = row // 2
+    outer = jnp.logical_or(row == 0, row == 3)
+    last = 3 * (1 - upper) * 2 + 1 - column
+    return outer, last
+
+
+def write_kernel(total, out, sems):
+    width = total.shape[2]
+    blocks = out.shape[1] // width
+    _, last = place()
+
+    def piece(k):
+        columns = pl.ds(pl.multiple_of((last + 1 + k) % blocks * width, width), width)
+        return pltpu.make_async_copy(total.at[k], out.at[:, columns], sems.at[k])
+
+    for k in range(blocks - 1):
+        piece(k).start()
+    for k in range(blocks - 1):
+        piece(k).wait()
+
+
+def write_most(total):
+    blocks, rows, width = total.shape
+    assets = (blocks + 1) * width
+    return pl.pallas_call(
+        write_kernel,
+        out_shape=jax.ShapeDtypeStruct((rows, assets), total.dtype),
+        in_specs=[pl.BlockSpec(memory_space=pltpu.VMEM)],
+        out_specs=pl.BlockSpec(memory_space=pltpu.HBM),
+        scratch_shapes=[pltpu.SemaphoreType.DMA((blocks,))],
+        compiler_params=pltpu.CompilerParams(vmem_limit_bytes=1024 * 1024),
+        cost_estimate=pl.CostEstimate(
+            flops=0, bytes_accessed=8 * rows * assets, transcendentals=0
+        ),
+    )(total)
+
+
+def finish_kernel(tail, left, from_x, from_z, held, out, stage, sems):
+    width, part = left.shape[0], from_x.shape[2]
+    outer, last = place()
+    late = jnp.logical_and(outer, lax.axis_index("tm") == 1)
+    start = pl.multiple_of(last * width, width)
+
+    @pl.when(jnp.logical_not(late))
+    def _():
+        columns = pl.ds(start, width)
+        copy = pltpu.make_async_copy(tail, out.at[:, columns], sems.at[0])
+        copy.start()
+        copy.wait()
+
+    @pl.when(late)
+    def _():
+        copies = []
+        for p in range(PIECES):
+            source = from_x if p < HALF else from_z
+            columns = pl.ds(pl.multiple_of(start + p * part, part), part)
+            stage[p] = tail[:, pl.ds(p * part, part)] + jnp.dot(
+                left[...], source[p % HALF], preferred_element_type=jnp.float32
+            )
+            copies.append(pltpu.make_async_copy(stage.at[p], out.at[:, columns], sems.at[p]))
+            copies[-1].start()
+        for copy in copies:
+            copy.wait()
+
+
+def finish(tail, left, from_x, from_z, held):
+    rows = tail.shape[0]
+    width, minutes = left.shape
+    vmem, hbm = pl.BlockSpec(memory_space=pltpu.VMEM), pl.BlockSpec(memory_space=pltpu.HBM)
+    return pl.pallas_call(
+        finish_kernel,
+        out_shape=jax.ShapeDtypeStruct(held.shape, held.dtype),
+        in_specs=[vmem, vmem, vmem, vmem, hbm],
+        out_specs=hbm,
+        scratch_shapes=[
+            pltpu.VMEM((PIECES, rows, width // PIECES), jnp.float32),
+            pltpu.SemaphoreType.DMA((PIECES,)),
+        ],
+        input_output_aliases={4: 0},
+        compiler_params=pltpu.CompilerParams(vmem_limit_bytes=10 * 1024 * 1024),
+        cost_estimate=pl.CostEstimate(
+            flops=2 * rows * width * minutes, bytes_accessed=4 * rows * width, transcendentals=0
+        ),
+    )(tail, left, from_x, from_z, held)
 
 
 def local_planned(returns, prior):
     minutes, width = returns.shape
     rows, assets = prior.shape
     part = width // PIECES
-    square, factor = powers_of(minutes)
-    slab = lax.axis_index("tm")
-    coef = jnp.stack([jnp.where(slab > 0, factor * factor, factor), factor])
     count = assets // width * PIECES
-    out = pl.pallas_call(
+    hbm, vmem = pl.BlockSpec(memory_space=pltpu.HBM), pl.BlockSpec(memory_space=pltpu.VMEM)
+    semaphores = [PIECES, assets // width]
+    semaphores += 2 * [3 * PIECES + HALF, 3 * PIECES + HALF, 2 * PIECES, count]
+    total, tail, left, hand = pl.pallas_call(
         kernel,
-        out_shape=pltpu.VMEM((rows, assets), jnp.float32),
-        in_specs=[
-            pl.BlockSpec(memory_space=pltpu.SMEM),
-            pl.BlockSpec(memory_space=pltpu.HBM),
-            pl.BlockSpec(memory_space=pltpu.HBM),
-            pl.BlockSpec(memory_space=pltpu.VMEM),
-        ],
-        out_specs=pl.BlockSpec(memory_space=pltpu.VMEM),
+        out_shape=(
+            pltpu.VMEM((assets // width - 1, rows, width), jnp.float32),
+            pltpu.VMEM((rows, width), jnp.float32),
+            pltpu.VMEM((width, minutes), jnp.bfloat16),
+            pltpu.HBM((HALF, minutes, part), jnp.bfloat16),
+        ),
+        in_specs=[hbm, hbm],
+        out_specs=(vmem, vmem, vmem, hbm),
         scratch_shapes=[
             pltpu.VMEM((count, minutes, part), jnp.bfloat16),
             pltpu.VMEM((count, minutes, part), jnp.bfloat16),
             pltpu.VMEM((width, minutes), jnp.bfloat16),
-            pltpu.VMEM((width, minutes), jnp.bfloat16),
-            pltpu.SemaphoreType.DMA((PIECES,)),
-            pltpu.SemaphoreType.DMA((assets // width,)),
-            pltpu.SemaphoreType.DMA((14,)),
-            pltpu.SemaphoreType.DMA((14,)),
-            pltpu.SemaphoreType.DMA((8,)),
-            pltpu.SemaphoreType.DMA((count,)),
-            pltpu.SemaphoreType.DMA((14,)),
-            pltpu.SemaphoreType.DMA((14,)),
-            pltpu.SemaphoreType.DMA((8,)),
-            pltpu.SemaphoreType.DMA((count,)),
+            *[pltpu.SemaphoreType.DMA((n,)) for n in semaphores],
         ],
         compiler_params=pltpu.CompilerParams(
-            collective_id=0, has_side_effects=True, vmem_limit_bytes=31457280
+            collective_id=0, has_side_effects=True, vmem_limit_bytes=29 * 1024 * 1024
         ),
-    )(coef, pltpu.with_memory_space_constraint(returns, pltpu.HBM), prior, square[None, :])
-    return out[None]
+    )(pltpu.with_memory_space_constraint(returns, pltpu.HBM), prior)
+    at = lambda row, column: (row * 2 + column) * 2 + 1
+    pairs_x = [(at(r, c), at(r, 1 - c)) for r in (0, 3) for c in (0, 1)]
+    pairs_z = [(at(n, c), at(r, c)) for r, n in ((0, 1), (3, 2)) for c in (0, 1)]
+    from_x = lax.ppermute(hand, ("assets", "tm"), pairs_x)
+    from_z = lax.ppermute(hand, ("assets", "tm"), pairs_z)
+    return finish(tail, left, from_x, from_z, write_most(total))[None]
 
 
 def solution(mesh):

time: 142 us -> 136 us (0.958)
  local copies, waits for them, and re-layouts: 11.7 us -> 0 us
  starting transfers between devices: 0 us -> 3.95 us
  Pallas kernels: 129 us -> 132 us
    unnamed x1 -> x0, local copies, waits for them, and re-layouts: 11.7 us -> none
    ppermute x0 -> x2, starting transfers between devices: none -> 3.95 us  [the longest x1 2.66 us: local_planned(): from_x = lax.ppermute(hand, ('assets', 'tm'), pairs_x)]
    pallas_call x1 -> x3, Pallas kernels: 129 us -> 132 us  [the longest x1 119 us: local_planned(): pl.pallas_call(kernel, out_shape=(pltpu.VMEM((assets // width - 1, rows,...]
  transfers between devices with their start and end apart: 0 -> 2, of which waited for: 0 -> 1; matrix products, arithmetic and copies ran while one was open for 0% -> 0% of each run, Pallas kernels for 0% -> 7%
where the time goes in v1:
time: 136 us
  Pallas kernels  132 us (97%)
  starting transfers between devices  3.95 us (3%)
    pallas_call x1, Pallas kernels, local_planned(): pl.pallas_call(kernel, out_shape=(pltpu.VMEM((assets // width - 1, rows,...  119 us
    pallas_call x1, Pallas kernels, write_most(): pl.pallas_call(write_kernel, out_shape=jax.ShapeDtypeStruct((rows, assets...  9.79 us
    pallas_call x1, Pallas kernels, finish(): pl.pallas_call(finish_kernel, out_shape=jax.ShapeDtypeStruct(held.shape,...  3.33 us
  transfers between devices with their start and end apart: 2, of which 1 were waited for; matrix products, arithmetic and copies ran while one was open for 0% of the time, Pallas kernels for 7%

profile of v1, /device:TPU:1, one launch (start us, length us, event | category | flops | bytes accessed | tf_op | source)
XLA Modules:
  0.0 136.2 jit_solution(7443911588643854276)
XLA Ops:
  0.0 118.6 %shard_map.28 = (f32[7,1024,1024]{2,1,0:T(8,128)S(1)}, f32[1024,1024]{1,0:T(8,128)S(1)}, bf16[1024,768]{1,0:T(8,128)(2,1)S(1)}, bf16[2,768,256]{2,1,0:T(8,128)(2,1)}) custom-call(bf16[768,1024]{1,0:T(8,128)(2,1)} %returns.1, f32[1024,8192]{1,0:T(8,128)} %prior.1), custom_call_target="tpu_custom_call" | custom-call | tf_op jit(solution)/shard_map/pallas_call | solution.py:410
  118.6 1.3 collective-permute-start.1
  119.9 2.7 %collective-permute-start = (bf16[2,768,256]{2,1,0:T(8,128)(2,1)}, bf16[2,768,256]{2,1,0:T(8,128)(2,1)S(1)}, u32[]{:S(2)}, u32[]{:S(2)}) collective-permute-start(bf16[2,768,256]{2,1,0:T(8,128)(2,1)} %get-tuple-element.11), channel_id=1, source_target_pairs={{1,3},{3,1},{13,15},{15,13},{17,19},{19,17},{29,31},{31,29}} | collective-permute-start | bytes 2359304 | tf_op jit(solution)/shard_map/ppermute | solution.py:433
  122.6 9.8 %shard_map.29.held = f32[1024,8192]{1,0:T(8,128)} custom-call(f32[7,1024,1024]{2,1,0:T(8,128)S(1)} %get-tuple-element.12.total), custom_call_target="tpu_custom_call" | custom-call | bytes 67108864 | tf_op jit(solution)/shard_map/pallas_call | solution.py:340
  132.4 0.0 collective-permute-done.1.from_z
  132.4 0.5 collective-permute-done.from_x
  132.9 3.3 %shard_map.30 = f32[1024,8192]{1,0:T(8,128)} custom-call(f32[1024,1024]{1,0:T(8,128)S(1)} %get-tuple-element.9.tail, bf16[1024,768]{1,0:T(8,128)(2,1)S(1)} %get-tuple-element.10.left, bf16[2,768,256]{2,1,0:T(8,128)(2,1)S(1)} %collective-permute-done.from_x, bf16[2,768,256]{2,1,0:T(8,128)(2,1)S(1)} %collective-permute-done.1.from_z, ...), custom_call_target="tpu_custom_call", output_to_operand_aliasing={{}: (4, {})} | custom-call | flops 1610612736 | bytes 4194304 | tf_op jit(solution)/shard_map/pallas_call | solution.py:385
Async XLA Ops:
  118.6 13.8 %collective-permute-start.1 = (bf16[2,768,256]{2,1,0:T(8,128)(2,1)}, bf16[2,768,256]{2,1,0:T(8,128)(2,1)S(1)}, u32[]{:S(2)}, u32[]{:S(2)}) collective-permute-start(bf16[2,768,256]{2,1,0:T(8,128)(2,1)} %get-tuple-element.11), channel_id=1, source_target_pairs={{5,1},{7,3},{9,13},{11,15},{21,17},{23,19},{25,29},{27,31}} | collective-permute-start | bytes 2359304 | tf_op jit(solution)/shard_map/ppermute | solution.py:434
  119.9 12.9 %collective-permute-start = (bf16[2,768,256]{2,1,0:T(8,128)(2,1)}, bf16[2,768,256]{2,1,0:T(8,128)(2,1)S(1)}, u32[]{:S(2)}, u32[]{:S(2)}) collective-permute-start(bf16[2,768,256]{2,1,0:T(8,128)(2,1)} %get-tuple-element.11), channel_id=1, source_target_pairs={{1,3},{3,1},{13,15},{15,13},{17,19},{19,17},{29,31},{31,29}} | collective-permute-start | bytes 2359304 | tf_op jit(solution)/shard_map/ppermute | solution.py:433

commit v2 on v1

--- a/solution.py
+++ b/solution.py
@@ -44,7 +44,7 @@
 
 def kernel(
     returns, prior, total, tail, left, hand, mine, early, left_early,
-    load_sem, prior_sem, x_send, z_send, c_send, f_send, x_recv, z_recv, c_recv, f_recv
+    load_sem, prior_sem, send_sem, x_recv, z_recv, c_recv, f_recv
 ):
     minutes, width = returns.shape
     part = width // PIECES
@@ -90,23 +90,27 @@
         return mine.at[j * PIECES + p]
 
     def send_x(source, j, p, k):
-        remote(source, slot(j, p), x_send.at[k], x_recv.at[k], {"assets": across}).start()
+        remote(source, slot(j, p), send_sem.at[0], x_recv.at[k], {"assets": across}).start()
 
     def send_z(source, j, p, k):
-        remote(source, slot(j, p), z_send.at[k], z_recv.at[k], {"assets": beside}).start()
+        remote(source, slot(j, p), send_sem.at[1], z_recv.at[k], {"assets": beside}).start()
 
     def send_c(source, j, p, k):
-        remote(source, slot(j, p), c_send.at[k], c_recv.at[k], {"assets": centre}).start()
+        remote(source, slot(j, p), send_sem.at[2], c_recv.at[k], {"assets": centre}).start()
 
     def hand_on(source, j, p):
         k = j * PIECES + p
 
         @pl.when(first)
         def _():
-            remote(source, early.at[k], f_send.at[k], f_recv.at[k], {"tm": 1 - core}).start()
+            remote(source, early.at[k], send_sem.at[3], f_recv.at[k], {"tm": 1 - core}).start()
 
     def wait_recv(sem):
         pltpu.make_async_copy(mine.at[0], mine.at[0], sem).wait()
+
+    def wait_all(sem, count):
+        pieces = mine.at[pl.ds(0, count)]
+        pltpu.make_async_copy(pieces, pieces, sem).wait()
 
     def got(sem, j, p):
         wait_recv(sem)
@@ -123,7 +127,7 @@
             send_c(own(p), me, p, p)
 
         hand_on(own(p), me, p)
-        pltpu.make_async_copy(own(p), slot(me, p), load_sem.at[p]).start()
+        pltpu.make_async_copy(own(p), slot(me, p), load_sem.at[0]).start()
 
     blocks = prior.shape[1] // width
     last = block(3, other)
@@ -132,10 +136,10 @@
     def prior_copy(k):
         j = (last + 1 + k) % blocks
         columns = pl.ds(pl.multiple_of(j * width, width), width)
-        return pltpu.make_async_copy(prior.at[:, columns], total.at[k], prior_sem.at[k])
+        return pltpu.make_async_copy(prior.at[:, columns], total.at[k], prior_sem.at[0])
 
     tail_copy = pltpu.make_async_copy(
-        prior.at[:, pl.ds(pl.multiple_of(last * width, width), width)], tail, prior_sem.at[blocks - 1]
+        prior.at[:, pl.ds(pl.multiple_of(last * width, width), width)], tail, prior_sem.at[1]
     )
 
     def start_prior(k, carry):
@@ -146,7 +150,6 @@
     tail_copy.start()
 
     def prepare(p, carry):
-        pltpu.make_async_copy(own(p), slot(me, p), load_sem.at[p]).wait()
         rows = pl.ds(pl.multiple_of(p * part, part), part)
         turned = mine[me * PIECES + p].astype(jnp.float32).T
         left[rows, :] = (turned * square).astype(jnp.bfloat16)
@@ -160,17 +163,14 @@
 
         return carry
 
+    wait_all(load_sem.at[0], PIECES)
     lax.fori_loop(0, PIECES, prepare, 0)
 
-    def wait_prior(j, carry):
-        prior_copy(j).wait()
-        return carry
-
-    lax.fori_loop(0, blocks - 1, wait_prior, 0)
+    pltpu.make_async_copy(total, total, prior_sem.at[0]).wait()
     tail_copy.wait()
 
     def keep(j, p, k):
-        return pltpu.make_async_copy(slot(j, p), hand.at[k], load_sem.at[k])
+        return pltpu.make_async_copy(slot(j, p), hand.at[k], load_sem.at[0])
 
     def product(target, j, p, arrived=True, whole=True):
         k = j * PIECES + p
@@ -280,34 +280,21 @@
 
         lax.fori_loop(0, PIECES, end, 0)
 
-    def wait_send(sem):
-        pltpu.make_async_copy(mine.at[0], mine.at[0], sem).wait()
-
-    def waits(sems, start, stop):
-        def turn(k, carry):
-            wait_send(sems.at[k])
-            return carry
-
-        lax.fori_loop(start, stop, turn, 0)
-
-    waits(x_send, 0, 3 * PIECES)
-    waits(z_send, 0, 2 * PIECES)
+    @pl.when(outer)
+    def _():
+        wait_all(send_sem.at[1], 2 * PIECES)
+        pl.when(first)(lambda: wait_all(send_sem.at[0], 3 * PIECES + HALF))
+        pl.when(second)(lambda: wait_all(send_sem.at[0], 3 * PIECES))
 
     @pl.when(inner)
     def _():
-        waits(z_send, 2 * PIECES, 3 * PIECES)
-        waits(c_send, 0, 2 * PIECES)
-
-    @pl.when(first)
-    def _():
-        pl.when(outer)(lambda: waits(x_send, 3 * PIECES, 3 * PIECES + HALF))
-        pl.when(inner)(lambda: waits(z_send, 3 * PIECES, 3 * PIECES + HALF))
-        waits(f_send, 0, blocks * PIECES)
-
-    @pl.when(second)
-    def _():
-        for k in range(HALF):
-            keep(0, 0, k).wait()
+        wait_all(send_sem.at[0], 3 * PIECES)
+        wait_all(send_sem.at[2], 2 * PIECES)
+        pl.when(first)(lambda: wait_all(send_sem.at[1], 3 * PIECES + HALF))
+        pl.when(second)(lambda: wait_all(send_sem.at[1], 3 * PIECES))
+
+    pl.when(first)(lambda: wait_all(send_sem.at[3], blocks * PIECES))
+    pl.when(second)(lambda: wait_all(load_sem.at[0], HALF))
 
 
 def place():
@@ -405,8 +392,7 @@
     part = width // PIECES
     count = assets // width * PIECES
     hbm, vmem = pl.BlockSpec(memory_space=pltpu.HBM), pl.BlockSpec(memory_space=pltpu.VMEM)
-    semaphores = [PIECES, assets // width]
-    semaphores += 2 * [3 * PIECES + HALF, 3 * PIECES + HALF, 2 * PIECES, count]
+    semaphores = [1, 2, 4, 3 * PIECES + HALF, 3 * PIECES + HALF, 2 * PIECES, count]
     total, tail, left, hand = pl.pallas_call(
         kernel,
         out_shape=(

time: 136 us -> 136 us (level)
  no operation moved by 1% of the time
where the time goes in v2:
time: 136 us; the launch traced here: 135 us
  Pallas kernels  131 us (96%)
  starting transfers between devices  3.95 us (3%)
    pallas_call x1, Pallas kernels, local_planned(): pl.pallas_call(kernel, out_shape=(pltpu.VMEM((assets // width - 1, rows,...  118 us
    pallas_call x1, Pallas kernels, write_most(): pl.pallas_call(write_kernel, out_shape=jax.ShapeDtypeStruct((rows, assets...  9.79 us
    pallas_call x1, Pallas kernels, finish(): pl.pallas_call(finish_kernel, out_shape=jax.ShapeDtypeStruct(held.shape,...  3.33 us
  transfers between devices with their start and end apart: 2, of which 1 were waited for; matrix products, arithmetic and copies ran while one was open for 0% of the time, Pallas kernels for 7%

profile of v2, /device:TPU:1, one launch (start us, length us, event | category | flops | bytes accessed | tf_op | source)
XLA Modules:
  0.0 135.4 jit_solution(11433592799666430071)
XLA Ops:
  0.0 117.8 %shard_map.28 = (f32[7,1024,1024]{2,1,0:T(8,128)S(1)}, f32[1024,1024]{1,0:T(8,128)S(1)}, bf16[1024,768]{1,0:T(8,128)(2,1)S(1)}, bf16[2,768,256]{2,1,0:T(8,128)(2,1)}) custom-call(bf16[768,1024]{1,0:T(8,128)(2,1)} %returns.1, f32[1024,8192]{1,0:T(8,128)} %prior.1), custom_call_target="tpu_custom_call" | custom-call | tf_op jit(solution)/shard_map/pallas_call | solution.py:396
  117.9 1.3 collective-permute-start.1
  119.2 2.7 %collective-permute-start = (bf16[2,768,256]{2,1,0:T(8,128)(2,1)}, bf16[2,768,256]{2,1,0:T(8,128)(2,1)S(1)}, u32[]{:S(2)}, u32[]{:S(2)}) collective-permute-start(bf16[2,768,256]{2,1,0:T(8,128)(2,1)} %get-tuple-element.11), channel_id=1, source_target_pairs={{1,3},{3,1},{13,15},{15,13},{17,19},{19,17},{29,31},{31,29}} | collective-permute-start | bytes 2359304 | tf_op jit(solution)/shard_map/ppermute | solution.py:419
  121.8 9.8 %shard_map.29.held = f32[1024,8192]{1,0:T(8,128)} custom-call(f32[7,1024,1024]{2,1,0:T(8,128)S(1)} %get-tuple-element.12.total), custom_call_target="tpu_custom_call" | custom-call | bytes 67108864 | tf_op jit(solution)/shard_map/pallas_call | solution.py:327
  131.6 0.0 collective-permute-done.1.from_z
  131.6 0.5 collective-permute-done.from_x
  132.1 3.3 %shard_map.30 = f32[1024,8192]{1,0:T(8,128)} custom-call(f32[1024,1024]{1,0:T(8,128)S(1)} %get-tuple-element.9.tail, bf16[1024,768]{1,0:T(8,128)(2,1)S(1)} %get-tuple-element.10.left, bf16[2,768,256]{2,1,0:T(8,128)(2,1)S(1)} %collective-permute-done.from_x, bf16[2,768,256]{2,1,0:T(8,128)(2,1)S(1)} %collective-permute-done.1.from_z, ...), custom_call_target="tpu_custom_call", output_to_operand_aliasing={{}: (4, {})} | custom-call | flops 1610612736 | bytes 4194304 | tf_op jit(solution)/shard_map/pallas_call | solution.py:372
Async XLA Ops:
  117.9 13.8 %collective-permute-start.1 = (bf16[2,768,256]{2,1,0:T(8,128)(2,1)}, bf16[2,768,256]{2,1,0:T(8,128)(2,1)S(1)}, u32[]{:S(2)}, u32[]{:S(2)}) collective-permute-start(bf16[2,768,256]{2,1,0:T(8,128)(2,1)} %get-tuple-element.11), channel_id=1, source_target_pairs={{5,1},{7,3},{9,13},{11,15},{21,17},{23,19},{25,29},{27,31}} | collective-permute-start | bytes 2359304 | tf_op jit(solution)/shard_map/ppermute | solution.py:420
  119.2 12.9 %collective-permute-start = (bf16[2,768,256]{2,1,0:T(8,128)(2,1)}, bf16[2,768,256]{2,1,0:T(8,128)(2,1)S(1)}, u32[]{:S(2)}, u32[]{:S(2)}) collective-permute-start(bf16[2,768,256]{2,1,0:T(8,128)(2,1)} %get-tuple-element.11), channel_id=1, source_target_pairs={{1,3},{3,1},{13,15},{15,13},{17,19},{19,17},{29,31},{31,29}} | collective-permute-start | bytes 2359304 | tf_op jit(solution)/shard_map/ppermute | solution.py:419

commit v3 on v2

--- a/solution.py
+++ b/solution.py
@@ -43,7 +43,7 @@
 
 
 def kernel(
-    returns, prior, total, tail, left, hand, mine, early, left_early,
+    returns, prior, total, tail, left, left_early, hand, rest, mine, early,
     load_sem, prior_sem, send_sem, x_recv, z_recv, c_recv, f_recv
 ):
     minutes, width = returns.shape
@@ -172,7 +172,7 @@
     def keep(j, p, k):
         return pltpu.make_async_copy(slot(j, p), hand.at[k], load_sem.at[0])
 
-    def product(target, j, p, arrived=True, whole=True):
+    def product(target, j, p, arrived=True):
         k = j * PIECES + p
         columns = pl.ds(pl.multiple_of(p * part, part), part)
 
@@ -189,8 +189,7 @@
             now = factor * factor * target[:, columns] + jnp.dot(
                 left_early[...], early[k], preferred_element_type=jnp.float32
             )
-            if whole:
-                now += jnp.dot(left[...], mine[k], preferred_element_type=jnp.float32)
+            now += jnp.dot(left[...], mine[k], preferred_element_type=jnp.float32)
             target[:, columns] = now
 
     def own_product(p, carry):
@@ -227,19 +226,33 @@
 
         lax.fori_loop(0, 3 * PIECES, turn, 0)
 
-        def end(p, carry):
+        @pl.when(first)
+        def _():
             j = block(3, other)
 
-            @pl.when(first)
-            def _():
-                got(x_recv.at[3 * PIECES + p], j, p)
-                got(z_recv.at[3 * PIECES + p], j, HALF + p)
-
-            product(tail, j, p, whole=False)
-            product(tail, j, HALF + p, whole=False)
-            return carry
-
-        lax.fori_loop(0, HALF, end, 0)
+            def end(i, carry):
+                for sem, p in ((x_recv, i), (z_recv, HALF + i)):
+                    wait_recv(sem.at[3 * PIECES + i])
+                    pltpu.make_async_copy(slot(j, p), rest.at[p], load_sem.at[p]).start()
+                for p in (i, HALF + i):
+                    columns = pl.ds(pl.multiple_of(p * part, part), part)
+                    tail[:, columns] = factor * tail[:, columns] + jnp.dot(
+                        left[...], mine[j * PIECES + p], preferred_element_type=jnp.float32
+                    )
+                return carry
+
+            lax.fori_loop(0, HALF, end, 0)
+            for p in range(PIECES):
+                wait_recv(load_sem.at[p])
+
+        @pl.when(second)
+        def _():
+            def fade(p, carry):
+                columns = pl.ds(pl.multiple_of(p * part, part), part)
+                tail[:, columns] = factor * factor * tail[:, columns]
+                return carry
+
+            lax.fori_loop(0, PIECES, fade, 0)
 
     @pl.when(inner)
     def _():
@@ -293,7 +306,8 @@
         pl.when(first)(lambda: wait_all(send_sem.at[1], 3 * PIECES + HALF))
         pl.when(second)(lambda: wait_all(send_sem.at[1], 3 * PIECES))
 
-    pl.when(first)(lambda: wait_all(send_sem.at[3], blocks * PIECES))
+    pl.when(jnp.logical_and(first, outer))(lambda: wait_all(send_sem.at[3], (blocks - 1) * PIECES))
+    pl.when(jnp.logical_and(first, inner))(lambda: wait_all(send_sem.at[3], blocks * PIECES))
     pl.when(second)(lambda: wait_all(load_sem.at[0], HALF))
 
 
@@ -337,7 +351,7 @@
     )(total)
 
 
-def finish_kernel(tail, left, from_x, from_z, held, out, stage, sems):
+def finish_kernel(tail, left, left_early, from_x, from_z, from_core, held, out, stage, sems):
     width, part = left.shape[0], from_x.shape[2]
     outer, last = place()
     late = jnp.logical_and(outer, lax.axis_index("tm") == 1)
@@ -356,8 +370,10 @@
         for p in range(PIECES):
             source = from_x if p < HALF else from_z
             columns = pl.ds(pl.multiple_of(start + p * part, part), part)
-            stage[p] = tail[:, pl.ds(p * part, part)] + jnp.dot(
-                left[...], source[p % HALF], preferred_element_type=jnp.float32
+            stage[p] = (
+                tail[:, pl.ds(p * part, part)]
+                + jnp.dot(left[...], source[p % HALF], preferred_element_type=jnp.float32)
+                + jnp.dot(left_early[...], from_core[p], preferred_element_type=jnp.float32)
             )
             copies.append(pltpu.make_async_copy(stage.at[p], out.at[:, columns], sems.at[p]))
             copies[-1].start()
@@ -365,25 +381,25 @@
             copy.wait()
 
 
-def finish(tail, left, from_x, from_z, held):
+def finish(tail, left, left_early, from_x, from_z, from_core, held):
     rows = tail.shape[0]
     width, minutes = left.shape
     vmem, hbm = pl.BlockSpec(memory_space=pltpu.VMEM), pl.BlockSpec(memory_space=pltpu.HBM)
     return pl.pallas_call(
         finish_kernel,
         out_shape=jax.ShapeDtypeStruct(held.shape, held.dtype),
-        in_specs=[vmem, vmem, vmem, vmem, hbm],
+        in_specs=[vmem] * 6 + [hbm],
         out_specs=hbm,
         scratch_shapes=[
             pltpu.VMEM((PIECES, rows, width // PIECES), jnp.float32),
             pltpu.SemaphoreType.DMA((PIECES,)),
         ],
-        input_output_aliases={4: 0},
+        input_output_aliases={6: 0},
         compiler_params=pltpu.CompilerParams(vmem_limit_bytes=10 * 1024 * 1024),
         cost_estimate=pl.CostEstimate(
             flops=2 * rows * width * minutes, bytes_accessed=4 * rows * width, transcendentals=0
         ),
-    )(tail, left, from_x, from_z, held)
+    )(tail, left, left_early, from_x, from_z, from_core, held)
 
 
 def local_planned(returns, prior):
@@ -392,33 +408,36 @@
     part = width // PIECES
     count = assets // width * PIECES
     hbm, vmem = pl.BlockSpec(memory_space=pltpu.HBM), pl.BlockSpec(memory_space=pltpu.VMEM)
-    semaphores = [1, 2, 4, 3 * PIECES + HALF, 3 * PIECES + HALF, 2 * PIECES, count]
-    total, tail, left, hand = pl.pallas_call(
+    semaphores = [PIECES, 2, 4, 3 * PIECES + HALF, 3 * PIECES + HALF, 2 * PIECES, count]
+    total, tail, left, left_early, hand, rest = pl.pallas_call(
         kernel,
         out_shape=(
             pltpu.VMEM((assets // width - 1, rows, width), jnp.float32),
             pltpu.VMEM((rows, width), jnp.float32),
             pltpu.VMEM((width, minutes), jnp.bfloat16),
+            pltpu.VMEM((width, minutes), jnp.bfloat16),
             pltpu.HBM((HALF, minutes, part), jnp.bfloat16),
+            pltpu.HBM((PIECES, minutes, part), jnp.bfloat16),
         ),
         in_specs=[hbm, hbm],
-        out_specs=(vmem, vmem, vmem, hbm),
+        out_specs=(vmem, vmem, vmem, vmem, hbm, hbm),
         scratch_shapes=[
             pltpu.VMEM((count, minutes, part), jnp.bfloat16),
             pltpu.VMEM((count, minutes, part), jnp.bfloat16),
-            pltpu.VMEM((width, minutes), jnp.bfloat16),
             *[pltpu.SemaphoreType.DMA((n,)) for n in semaphores],
         ],
         compiler_params=pltpu.CompilerParams(
-            collective_id=0, has_side_effects=True, vmem_limit_bytes=29 * 1024 * 1024
+            collective_id=0, has_side_effects=True, vmem_limit_bytes=28 * 1024 * 1024
         ),
     )(pltpu.with_memory_space_constraint(returns, pltpu.HBM), prior)
-    at = lambda row, column: (row * 2 + column) * 2 + 1
-    pairs_x = [(at(r, c), at(r, 1 - c)) for r in (0, 3) for c in (0, 1)]
-    pairs_z = [(at(n, c), at(r, c)) for r, n in ((0, 1), (3, 2)) for c in (0, 1)]
+    at = lambda row, column, core: (row * 2 + column) * 2 + core
+    pairs_x = [(at(r, c, 1), at(r, 1 - c, 1)) for r in (0, 3) for c in (0, 1)]
+    pairs_z = [(at(n, c, 1), at(r, c, 1)) for r, n in ((0, 1), (3, 2)) for c in (0, 1)]
+    pairs_core = [(at(r, c, 0), at(r, c, 1)) for r in (0, 3) for c in (0, 1)]
     from_x = lax.ppermute(hand, ("assets", "tm"), pairs_x)
     from_z = lax.ppermute(hand, ("assets", "tm"), pairs_z)
-    return finish(tail, left, from_x, from_z, write_most(total))[None]
+    from_core = lax.ppermute(rest, ("assets", "tm"), pairs_core)
+    return finish(tail, left, left_early, from_x, from_z, from_core, write_most(total))[None]
 
 
 def solution(mesh):

time: 136 us -> 132 us (0.971)
  Pallas kernels: 131 us -> 126 us
    pallas_call x1, Pallas kernels: 118 us -> 111 us  [local_planned(): pl.pallas_call(kernel, out_shape=(pltpu.VMEM((assets // width - 1, rows,...]
    pallas_call x1, Pallas kernels: 3.33 us -> 4.95 us  [finish(): pl.pallas_call(finish_kernel, out_shape=jax.ShapeDtypeStruct(held.shape,...]
  transfers between devices with their start and end apart: 2 -> 3, of which waited for: 1 -> 1; matrix products, arithmetic and copies ran while one was open for 0% -> 0% of each run, Pallas kernels for 7% -> 7%
where the time goes in v3:
time: 132 us; the launch traced here: 131 us
  Pallas kernels  126 us (95%)
  starting transfers between devices  4.83 us (4%)
    pallas_call x1, Pallas kernels, local_planned(): pl.pallas_call(kernel, out_shape=(pltpu.VMEM((assets // width - 1, rows,...  111 us
    pallas_call x1, Pallas kernels, write_most(): pl.pallas_call(write_kernel, out_shape=jax.ShapeDtypeStruct((rows, assets...  9.79 us
    pallas_call x1, Pallas kernels, finish(): pl.pallas_call(finish_kernel, out_shape=jax.ShapeDtypeStruct(held.shape,...  4.95 us
  transfers between devices with their start and end apart: 3, of which 1 were waited for; matrix products, arithmetic and copies ran while one was open for 0% of the time, Pallas kernels for 7%

profile of v3, /device:TPU:1, one launch (start us, length us, event | category | flops | bytes accessed | tf_op | source)
XLA Modules:
  0.0 131.3 jit_solution(10636477301280751930)
XLA Ops:
  0.0 110.8 %shard_map.28 = (f32[7,1024,1024]{2,1,0:T(8,128)S(1)}, f32[1024,1024]{1,0:T(8,128)S(1)}, bf16[1024,768]{1,0:T(8,128)(2,1)S(1)}, bf16[1024,768]{1,0:T(8,128)(2,1)...) custom-call(bf16[768,1024]{1,0:T(8,128)(2,1)} %returns.1, f32[1024,8192]{1,0:T(8,128)} %prior.1), custom_call_target="tpu_custom_call" | custom-call | tf_op jit(solution)/shard_map/pallas_call | solution.py:412
  110.8 1.3 collective-permute-start.2
  112.1 1.3 collective-permute-start.1
  113.4 2.2 %collective-permute-start = (bf16[2,768,256]{2,1,0:T(8,128)(2,1)}, bf16[2,768,256]{2,1,0:T(8,128)(2,1)S(1)}, u32[]{:S(2)}, u32[]{:S(2)}) collective-permute-start(bf16[2,768,256]{2,1,0:T(8,128)(2,1)} %get-tuple-element.14), channel_id=1, source_target_pairs={{1,3},{3,1},{13,15},{15,13},{17,19},{19,17},{29,31},{31,29}} | collective-permute-start | bytes 2359304 | tf_op jit(solution)/shard_map/ppermute | solution.py:437
  115.7 9.8 %shard_map.29.held = f32[1024,8192]{1,0:T(8,128)} custom-call(f32[7,1024,1024]{2,1,0:T(8,128)S(1)} %get-tuple-element.16.total), custom_call_target="tpu_custom_call" | custom-call | bytes 67108864 | tf_op jit(solution)/shard_map/pallas_call | solution.py:341
  125.5 0.0 collective-permute-done.1.from_z
  125.5 0.9 collective-permute-done.from_x
  126.3 0.0 collective-permute-done.2.from_core
  126.4 4.9 %shard_map.30 = f32[1024,8192]{1,0:T(8,128)} custom-call(f32[1024,1024]{1,0:T(8,128)S(1)} %get-tuple-element.11.tail, bf16[1024,768]{1,0:T(8,128)(2,1)S(1)} %get-tuple-element.12.left, bf16[1024,768]{1,0:T(8,128)(2,1)S(1)} %get-tuple-element.13.left_early, bf16[2,768,256]{2,1,0:T(8,128)(2,1)S(1)} %collective-permute-done.from_x, ...), custom_call_target="tpu_custom_call", output_to_operand_aliasing={{}: (6, {})} | custom-call | flops 1610612736 | bytes 4194304 | tf_op jit(solution)/shard_map/pallas_call | solution.py:388
Async XLA Ops:
  110.8 15.5 %collective-permute-start.2 = (bf16[4,768,256]{2,1,0:T(8,128)(2,1)}, bf16[4,768,256]{2,1,0:T(8,128)(2,1)S(1)}, u32[]{:S(2)}, u32[]{:S(2)}) collective-permute-start(bf16[4,768,256]{2,1,0:T(8,128)(2,1)} %get-tuple-element.15), channel_id=1, source_target_pairs={{0,1},{2,3},{12,13},{14,15},{16,17},{18,19},{28,29},{30,31}} | collective-permute-start | bytes 4718600 | tf_op jit(solution)/shard_map/ppermute | solution.py:439
  112.1 13.4 %collective-permute-start.1 = (bf16[2,768,256]{2,1,0:T(8,128)(2,1)}, bf16[2,768,256]{2,1,0:T(8,128)(2,1)S(1)}, u32[]{:S(2)}, u32[]{:S(2)}) collective-permute-start(bf16[2,768,256]{2,1,0:T(8,128)(2,1)} %get-tuple-element.14), channel_id=1, source_target_pairs={{5,1},{7,3},{9,13},{11,15},{21,17},{23,19},{25,29},{27,31}} | collective-permute-start | bytes 2359304 | tf_op jit(solution)/shard_map/ppermute | solution.py:438
  113.4 12.9 %collective-permute-start = (bf16[2,768,256]{2,1,0:T(8,128)(2,1)}, bf16[2,768,256]{2,1,0:T(8,128)(2,1)S(1)}, u32[]{:S(2)}, u32[]{:S(2)}) collective-permute-start(bf16[2,768,256]{2,1,0:T(8,128)(2,1)} %get-tuple-element.14), channel_id=1, source_target_pairs={{1,3},{3,1},{13,15},{15,13},{17,19},{19,17},{29,31},{31,29}} | collective-permute-start | bytes 2359304 | tf_op jit(solution)/shard_map/ppermute | solution.py:437

commit v4 on v3

--- a/solution.py
+++ b/solution.py
@@ -146,8 +146,6 @@
         prior_copy(k).start()
         return carry
 
-    lax.fori_loop(0, blocks - 1, start_prior, 0)
-    tail_copy.start()
 
     def prepare(p, carry):
         rows = pl.ds(pl.multiple_of(p * part, part), part)
@@ -164,6 +162,8 @@
         return carry
 
     wait_all(load_sem.at[0], PIECES)
+    lax.fori_loop(0, blocks - 1, start_prior, 0)
+    tail_copy.start()
     lax.fori_loop(0, PIECES, prepare, 0)
 
     pltpu.make_async_copy(total, total, prior_sem.at[0]).wait()
@@ -230,18 +230,15 @@
         def _():
             j = block(3, other)
 
-            def end(i, carry):
+            for i in range(HALF):
                 for sem, p in ((x_recv, i), (z_recv, HALF + i)):
                     wait_recv(sem.at[3 * PIECES + i])
                     pltpu.make_async_copy(slot(j, p), rest.at[p], load_sem.at[p]).start()
                 for p in (i, HALF + i):
-                    columns = pl.ds(pl.multiple_of(p * part, part), part)
+                    columns = pl.ds(p * part, part)
                     tail[:, columns] = factor * tail[:, columns] + jnp.dot(
                         left[...], mine[j * PIECES + p], preferred_element_type=jnp.float32
                     )
-                return carry
-
-            lax.fori_loop(0, HALF, end, 0)
             for p in range(PIECES):
                 wait_recv(load_sem.at[p])
 

time: 132 us -> 132 us (level)
  no operation moved by 1% of the time
where the time goes in v4:
time: 132 us; the launch traced here: 131 us
  Pallas kernels  126 us (95%)
  starting transfers between devices  4.83 us (4%)
    pallas_call x1, Pallas kernels, local_planned(): pl.pallas_call(kernel, out_shape=(pltpu.VMEM((assets // width - 1, rows,...  111 us
    pallas_call x1, Pallas kernels, write_most(): pl.pallas_call(write_kernel, out_shape=jax.ShapeDtypeStruct((rows, assets...  9.79 us
    pallas_call x1, Pallas kernels, finish(): pl.pallas_call(finish_kernel, out_shape=jax.ShapeDtypeStruct(held.shape,...  4.95 us
  transfers between devices with their start and end apart: 3, of which 1 were waited for; matrix products, arithmetic and copies ran while one was open for 0% of the time, Pallas kernels for 7%

profile of v4, /device:TPU:1, one launch (start us, length us, event | category | flops | bytes accessed | tf_op | source)
XLA Modules:
  0.0 131.3 jit_solution(9792576450849985021)
XLA Ops:
  0.0 110.8 %shard_map.28 = (f32[7,1024,1024]{2,1,0:T(8,128)S(1)}, f32[1024,1024]{1,0:T(8,128)S(1)}, bf16[1024,768]{1,0:T(8,128)(2,1)S(1)}, bf16[1024,768]{1,0:T(8,128)(2,1)...) custom-call(bf16[768,1024]{1,0:T(8,128)(2,1)} %returns.1, f32[1024,8192]{1,0:T(8,128)} %prior.1), custom_call_target="tpu_custom_call" | custom-call | tf_op jit(solution)/shard_map/pallas_call | solution.py:409
  110.8 1.3 collective-permute-start.2
  112.1 1.3 collective-permute-start.1
  113.4 2.2 %collective-permute-start = (bf16[2,768,256]{2,1,0:T(8,128)(2,1)}, bf16[2,768,256]{2,1,0:T(8,128)(2,1)S(1)}, u32[]{:S(2)}, u32[]{:S(2)}) collective-permute-start(bf16[2,768,256]{2,1,0:T(8,128)(2,1)} %get-tuple-element.14), channel_id=1, source_target_pairs={{1,3},{3,1},{13,15},{15,13},{17,19},{19,17},{29,31},{31,29}} | collective-permute-start | bytes 2359304 | tf_op jit(solution)/shard_map/ppermute | solution.py:434
  115.7 9.8 %shard_map.29.held = f32[1024,8192]{1,0:T(8,128)} custom-call(f32[7,1024,1024]{2,1,0:T(8,128)S(1)} %get-tuple-element.16.total), custom_call_target="tpu_custom_call" | custom-call | bytes 67108864 | tf_op jit(solution)/shard_map/pallas_call | solution.py:338
  125.5 0.0 collective-permute-done.1.from_z
  125.5 0.9 collective-permute-done.from_x
  126.3 0.0 collective-permute-done.2.from_core
  126.4 4.9 %shard_map.30 = f32[1024,8192]{1,0:T(8,128)} custom-call(f32[1024,1024]{1,0:T(8,128)S(1)} %get-tuple-element.11.tail, bf16[1024,768]{1,0:T(8,128)(2,1)S(1)} %get-tuple-element.12.left, bf16[1024,768]{1,0:T(8,128)(2,1)S(1)} %get-tuple-element.13.left_early, bf16[2,768,256]{2,1,0:T(8,128)(2,1)S(1)} %collective-permute-done.from_x, ...), custom_call_target="tpu_custom_call", output_to_operand_aliasing={{}: (6, {})} | custom-call | flops 1610612736 | bytes 4194304 | tf_op jit(solution)/shard_map/pallas_call | solution.py:385
Async XLA Ops:
  110.8 15.5 %collective-permute-start.2 = (bf16[4,768,256]{2,1,0:T(8,128)(2,1)}, bf16[4,768,256]{2,1,0:T(8,128)(2,1)S(1)}, u32[]{:S(2)}, u32[]{:S(2)}) collective-permute-start(bf16[4,768,256]{2,1,0:T(8,128)(2,1)} %get-tuple-element.15), channel_id=1, source_target_pairs={{0,1},{2,3},{12,13},{14,15},{16,17},{18,19},{28,29},{30,31}} | collective-permute-start | bytes 4718600 | tf_op jit(solution)/shard_map/ppermute | solution.py:436
  112.1 13.4 %collective-permute-start.1 = (bf16[2,768,256]{2,1,0:T(8,128)(2,1)}, bf16[2,768,256]{2,1,0:T(8,128)(2,1)S(1)}, u32[]{:S(2)}, u32[]{:S(2)}) collective-permute-start(bf16[2,768,256]{2,1,0:T(8,128)(2,1)} %get-tuple-element.14), channel_id=1, source_target_pairs={{5,1},{7,3},{9,13},{11,15},{21,17},{23,19},{25,29},{27,31}} | collective-permute-start | bytes 2359304 | tf_op jit(solution)/shard_map/ppermute | solution.py:435
  113.4 12.9 %collective-permute-start = (bf16[2,768,256]{2,1,0:T(8,128)(2,1)}, bf16[2,768,256]{2,1,0:T(8,128)(2,1)S(1)}, u32[]{:S(2)}, u32[]{:S(2)}) collective-permute-start(bf16[2,768,256]{2,1,0:T(8,128)(2,1)} %get-tuple-element.14), channel_id=1, source_target_pairs={{1,3},{3,1},{13,15},{15,13},{17,19},{19,17},{29,31},{31,29}} | collective-permute-start | bytes 2359304 | tf_op jit(solution)/shard_map/ppermute | solution.py:434

commit v5 on v4

--- a/solution.py
+++ b/solution.py
@@ -233,14 +233,13 @@
             for i in range(HALF):
                 for sem, p in ((x_recv, i), (z_recv, HALF + i)):
                     wait_recv(sem.at[3 * PIECES + i])
-                    pltpu.make_async_copy(slot(j, p), rest.at[p], load_sem.at[p]).start()
+                    pltpu.make_async_copy(slot(j, p), rest.at[p], load_sem.at[0]).start()
                 for p in (i, HALF + i):
                     columns = pl.ds(p * part, part)
                     tail[:, columns] = factor * tail[:, columns] + jnp.dot(
                         left[...], mine[j * PIECES + p], preferred_element_type=jnp.float32
                     )
-            for p in range(PIECES):
-                wait_recv(load_sem.at[p])
+            wait_all(load_sem.at[0], PIECES)
 
         @pl.when(second)
         def _():
@@ -405,7 +404,7 @@
     part = width // PIECES
     count = assets // width * PIECES
     hbm, vmem = pl.BlockSpec(memory_space=pltpu.HBM), pl.BlockSpec(memory_space=pltpu.VMEM)
-    semaphores = [PIECES, 2, 4, 3 * PIECES + HALF, 3 * PIECES + HALF, 2 * PIECES, count]
+    semaphores = [1, 2, 4, 3 * PIECES + HALF, 3 * PIECES + HALF, 2 * PIECES, count]
     total, tail, left, left_early, hand, rest = pl.pallas_call(
         kernel,
         out_shape=(

time: 132 us -> 132 us (level)
  no operation moved by 1% of the time
where the time goes in v5:
time: 132 us; the launch traced here: 131 us
  Pallas kernels  126 us (95%)
  starting transfers between devices  4.83 us (4%)
    pallas_call x1, Pallas kernels, local_planned(): pl.pallas_call(kernel, out_shape=(pltpu.VMEM((assets // width - 1, rows,...  111 us
    pallas_call x1, Pallas kernels, write_most(): pl.pallas_call(write_kernel, out_shape=jax.ShapeDtypeStruct((rows, assets...  9.79 us
    pallas_call x1, Pallas kernels, finish(): pl.pallas_call(finish_kernel, out_shape=jax.ShapeDtypeStruct(held.shape,...  4.94 us
  transfers between devices with their start and end apart: 3, of which 1 were waited for; matrix products, arithmetic and copies ran while one was open for 0% of the time, Pallas kernels for 7%

profile of v5, /device:TPU:1, one launch (start us, length us, event | category | flops | bytes accessed | tf_op | source)
XLA Modules:
  0.0 131.3 jit_solution(1735386724034291323)
XLA Ops:
  0.0 110.8 %shard_map.28 = (f32[7,1024,1024]{2,1,0:T(8,128)S(1)}, f32[1024,1024]{1,0:T(8,128)S(1)}, bf16[1024,768]{1,0:T(8,128)(2,1)S(1)}, bf16[1024,768]{1,0:T(8,128)(2,1)...) custom-call(bf16[768,1024]{1,0:T(8,128)(2,1)} %returns.1, f32[1024,8192]{1,0:T(8,128)} %prior.1), custom_call_target="tpu_custom_call" | custom-call | tf_op jit(solution)/shard_map/pallas_call | solution.py:408
  110.8 1.3 collective-permute-start.2
  112.1 1.3 collective-permute-start.1
  113.4 2.2 %collective-permute-start = (bf16[2,768,256]{2,1,0:T(8,128)(2,1)}, bf16[2,768,256]{2,1,0:T(8,128)(2,1)S(1)}, u32[]{:S(2)}, u32[]{:S(2)}) collective-permute-start(bf16[2,768,256]{2,1,0:T(8,128)(2,1)} %get-tuple-element.14), channel_id=1, source_target_pairs={{1,3},{3,1},{13,15},{15,13},{17,19},{19,17},{29,31},{31,29}} | collective-permute-start | bytes 2359304 | tf_op jit(solution)/shard_map/ppermute | solution.py:433
  115.6 9.8 %shard_map.29.held = f32[1024,8192]{1,0:T(8,128)} custom-call(f32[7,1024,1024]{2,1,0:T(8,128)S(1)} %get-tuple-element.16.total), custom_call_target="tpu_custom_call" | custom-call | bytes 67108864 | tf_op jit(solution)/shard_map/pallas_call | solution.py:337
  125.4 0.0 collective-permute-done.1.from_z
  125.4 0.9 collective-permute-done.from_x
  126.3 0.0 collective-permute-done.2.from_core
  126.3 4.9 %shard_map.30 = f32[1024,8192]{1,0:T(8,128)} custom-call(f32[1024,1024]{1,0:T(8,128)S(1)} %get-tuple-element.11.tail, bf16[1024,768]{1,0:T(8,128)(2,1)S(1)} %get-tuple-element.12.left, bf16[1024,768]{1,0:T(8,128)(2,1)S(1)} %get-tuple-element.13.left_early, bf16[2,768,256]{2,1,0:T(8,128)(2,1)S(1)} %collective-permute-done.from_x, ...), custom_call_target="tpu_custom_call", output_to_operand_aliasing={{}: (6, {})} | custom-call | flops 1610612736 | bytes 4194304 | tf_op jit(solution)/shard_map/pallas_call | solution.py:384
Async XLA Ops:
  110.8 15.5 %collective-permute-start.2 = (bf16[4,768,256]{2,1,0:T(8,128)(2,1)}, bf16[4,768,256]{2,1,0:T(8,128)(2,1)S(1)}, u32[]{:S(2)}, u32[]{:S(2)}) collective-permute-start(bf16[4,768,256]{2,1,0:T(8,128)(2,1)} %get-tuple-element.15), channel_id=1, source_target_pairs={{0,1},{2,3},{12,13},{14,15},{16,17},{18,19},{28,29},{30,31}} | collective-permute-start | bytes 4718600 | tf_op jit(solution)/shard_map/ppermute | solution.py:435
  112.1 13.4 %collective-permute-start.1 = (bf16[2,768,256]{2,1,0:T(8,128)(2,1)}, bf16[2,768,256]{2,1,0:T(8,128)(2,1)S(1)}, u32[]{:S(2)}, u32[]{:S(2)}) collective-permute-start(bf16[2,768,256]{2,1,0:T(8,128)(2,1)} %get-tuple-element.14), channel_id=1, source_target_pairs={{5,1},{7,3},{9,13},{11,15},{21,17},{23,19},{25,29},{27,31}} | collective-permute-start | bytes 2359304 | tf_op jit(solution)/shard_map/ppermute | solution.py:434
  113.4 12.9 %collective-permute-start = (bf16[2,768,256]{2,1,0:T(8,128)(2,1)}, bf16[2,768,256]{2,1,0:T(8,128)(2,1)S(1)}, u32[]{:S(2)}, u32[]{:S(2)}) collective-permute-start(bf16[2,768,256]{2,1,0:T(8,128)(2,1)} %get-tuple-element.14), channel_id=1, source_target_pairs={{1,3},{3,1},{13,15},{15,13},{17,19},{19,17},{29,31},{31,29}} | collective-permute-start | bytes 2359304 | tf_op jit(solution)/shard_map/ppermute | solution.py:433
